TPU v7x, 32 devices: a whole 2x2x4 slice. The times are simulated.
32 devices in a mesh: dp: 8 (over z, x), mp: 4 (over y, core).
Axes of the slice: x: 2, y: 2, z: 4, core: 2. Of those that a mesh axis runs over, the one named last changes fastest.
Arguments:
- acts: bfloat16 [6144, 4, 1984], P('dp', 'mp'), may hold values from -6 to 6
- grads: bfloat16 [6144, 4, 1984], P('dp', 'mp'), may hold values from -0.21875 to 0.21875
- error: bfloat16 [8, 4, 1984, 1984], P('dp', 'mp'), may hold values from -4 to 4
- momentum: float32 [4, 1984, 1984], P('mp', 'dp'), may hold values from -4 to 4
- q_start: float32 [4, 1984, 128], P('mp'), may hold values from -0.125 to 0.125
Outputs:
- error_next: bfloat16 [8, 4, 1984, 1984], P('dp', 'mp')
- momentum_next: float32 [4, 1984, 1984], P('mp', 'dp')
- q_next: float32 [4, 1984, 128], P('mp')
All inputs are finite; a program needn't handle non-finite values.
Results may differ from a plain program's by a relative error of at most 0.001.
Values sent between devices are 32-bit elements; how exact they have to be, the bound alone decides.
No kernel may reach another device: no remote copies, remote signals or barrier semaphores. Data moves between devices by JAX's collectives and lax.ppermute only.
A program may use at most 128 MiB of HBM per device.

v0:
```python
import jax
import jax.numpy as jnp
from jax import lax
from jax.sharding import PartitionSpec as P

D = 3968
PRECISE = lax.Precision.HIGHEST


def per_device(acts, grads, error, momentum, q_start):
    inputs = acts[:, 0, :]
    upstream = grads[:, 0, :]
    local_grad = lax.dot_general(
        inputs, upstream, (((0,), (0,)), ((), ())), preferred_element_type=jnp.float32
    )
    merged = local_grad + error[0, 0].astype(jnp.float32)
    warm_start = q_start[0]
    replicas = lax.axis_size("dp")
    owned_rows = momentum.shape[1]
    left_local = jnp.dot(merged, warm_start, precision=PRECISE)
    left_full = lax.psum(left_local, "dp")
    gram_matrix = jnp.dot(left_full.T, left_full, precision=PRECISE)
    cholesky_low = jnp.linalg.cholesky(gram_matrix)
    ortho_basis = lax.linalg.triangular_solve(
        cholesky_low, left_full, left_side=False, lower=True, transpose_a=True
    )
    basis_owned = lax.dynamic_slice_in_dim(
        ortho_basis, lax.axis_index("dp") * owned_rows, owned_rows, 0
    )
    right_local = lax.dot_general(merged, ortho_basis, (((0,), (0,)), ((), ())), precision=PRECISE)
    q_tile = lax.psum(right_local, "dp") / replicas
    norm_total = lax.psum(jnp.sum(q_tile * q_tile), "mp")
    rms_value = jnp.sqrt(norm_total / (D * D))
    decoded = jnp.dot(ortho_basis, q_tile.T, precision=PRECISE)
    error_next = (merged - decoded).astype(jnp.bfloat16)
    update = jnp.dot(basis_owned, q_tile.T, precision=PRECISE)
    momentum_next = 0.9 * momentum[0] + 0.1 * update / (rms_value + 1e-06)
    return (error_next[None, None], momentum_next[None], q_tile[None])


def solution(mesh):
    in_specs = (
        P("dp", "mp", None),
        P("dp", "mp", None),
        P("dp", "mp", None, None),
        P("mp", "dp", None),
        P("mp", None, None),
    )
    out_specs = (P("dp", "mp", None, None), P("mp", "dp", None), P("mp", None, None))
    return jax.shard_map(
        per_device, mesh=mesh, in_specs=in_specs, out_specs=out_specs, check_vma=False
    )
```

profile of v0, /device:TPU:0, one launch (start us, length us, event | category | flops | bytes accessed | tf_op | source)
XLA Modules:
  0.0 297.2 jit_solution(10708653032430564272)
XLA Ops:
  7.2 0.0 copy-start
  7.2 0.0 all-reduce.3.cloned.1.call-start
  7.2 1.8 copy-done
  9.0 9.3 %convert_add_fusion = f32[1984,1984]{1,0:T(8,128)S(1)} fusion(bf16[1,1,1984,1984]{3,2,1,0:T(8,128)(2,1)} %param.7, bf16[768,1,1984]{0,2,1:T(8,128)(2,1)S(1)} %copy-done, bf16[768,1,1984]{0,2,1:T(8,128)(2,1)} %param.5), kind=kOutput, calls=%fused_computation | convolution fusion | flops 6053961728 | bytes 29712384 | tf_op jit(solution)/shard_map/dot_general | solution.py:13
  18.4 0.0 copy-start.1
  18.4 5.6 %copy-done.1 = f32[1984,1984]{1,0:T(8,128)} copy-done((f32[1984,1984]{1,0:T(8,128)}, f32[1984,1984]{1,0:T(8,128)S(1)}, u32[]{:S(2)}) %copy-start.1) | copy-done | bytes 15745048
  24.0 15.3 %fusion.6 = f32[1984,128]{1,0:T(8,128)} fusion(f32[1984,1984]{1,0:T(8,128)S(1)} %convert_add_fusion, f32[1,1984,128]{2,1,0:T(8,128)} %param.9), kind=kOutput, calls=%fused_computation.9 | convolution fusion | flops 6046089216 | bytes 17776640 | tf_op jit(solution)/shard_map/dot_general | solution.py:20
  39.3 0.0 all-reduce.3.cloned.1.call-update
  39.3 0.2 all-reduce.5.cloned.1.call-start
  39.6 80.8 %all-reduce.3.cloned.1.call-done = f32[1984,128]{1,0:T(8,128)} async-done(((f32[1984,128]{1,0:T(8,128)}), f32[1984,128]{1,0:T(8,128)}) %all-reduce.3.cloned.1.call-update) | async-done | bytes 1015824 | tf_op jit(solution)/shard_map/psum | solution.py:21
  120.3 3.3 %fusion.20 = f32[128,128]{1,0:T(8,128)S(1)} fusion(f32[1984,128]{1,0:T(8,128)} %all-reduce.3.cloned.1.call-done), kind=kOutput, calls=%fused_computation.31 | convolution fusion | flops 390070272 | bytes 1081344 | tf_op jit(solution)/shard_map/dot_general | solution.py:22
  123.7 0.1 copy.8
  123.8 11.7 %cholesky.16 = f32[128,128]{1,0:T(8,128)S(1)} custom-call(f32[128,128]{1,0:T(8,128)S(1)} %fusion.16), custom_call_target="Cholesky" | custom-call | tf_op jit(solution)/shard_map/jit(cholesky)/cholesky | solution.py:23
  135.5 0.6 compare_reduce_fusion
  136.2 0.7 fusion.13
  136.9 9.8 %custom-call.6 = f32[1,128,128]{1,2,0:T(8,128)S(1)} custom-call(f32[1,128,128]{2,1,0:T(8,128)S(1)} %fusion.13), custom_call_target="InvertDiagBlocksLowerTriangular" | custom-call | tf_op jit(solution)/shard_map/triangular_solve | solution.py:24
  146.7 2.2 fusion.14
  148.8 0.0 copy-start.2
  148.8 1.0 copy-done.2
  149.8 29.9 %fusion.21 = f32[1984,128]{1,0:T(8,128)} fusion(f32[1984,1984]{1,0:T(8,128)} %copy-done.1, f32[1984,128]{1,0:T(8,128)S(1)} %fusion.14), kind=kOutput, calls=%fused_computation.32 | convolution fusion | flops 6046089216 | bytes 17776640 | tf_op jit(solution)/shard_map/dot_general | solution.py:30
  179.7 0.0 all-reduce.5.cloned.1.call-update
  179.7 77.0 %all-reduce.5.cloned.1.call-done = f32[1984,128]{1,0:T(8,128)} async-done(((f32[1984,128]{1,0:T(8,128)}), f32[1984,128]{1,0:T(8,128)}) %all-reduce.5.cloned.1.call-update) | async-done | bytes 1015824 | tf_op jit(solution)/shard_map/psum | solution.py:31
  256.8 3.0 multiply_bitcast_fusion
  259.7 6.5 %psum.23 = f32[]{:T(128)} all-reduce(f32[]{:T(128)} %get-tuple-element.4), channel_id=1, replica_groups=mesh['dp'=8,'mp'=4] {'mp'}, use_global_device_ids=true, to_apply=%region_5.6 | all-reduce | flops 1 | bytes 8 | tf_op jit(solution)/shard_map/psum | solution.py:32
  266.9 0.0 copy-start.3
  267.0 0.0 copy-start.4
  267.0 19.2 %fusion = bf16[1,1,1984,1984]{3,2,1,0:T(8,128)(2,1)} fusion(f32[1984,1984]{1,0:T(8,128)} %copy-done.1, f32[1984,128]{1,0:T(8,128)} %copy-done.2, f32[1984,128]{1,0:T(8,128)} %all-reduce.5.cloned.1.call-done), kind=kOutput, calls=%fused_computation.2 | convolution fusion | flops 6054215680 | bytes 25649152 | tf_op jit(solution)/shard_map/dot_general | solution.py:34
  286.1 0.0 copy-done.3
  286.1 0.0 copy-done.4
  286.1 4.2 %fusion.5 = f32[1,248,1984]{2,1,0:T(8,128)} fusion(f32[1,248,1984]{2,1,0:T(8,128)S(1)} %copy-done.4, f32[]{:T(128)S(6)} %add.32, f32[1984,128]{1,0:T(8,128)S(1)} %copy-done.3, f32[1984,128]{1,0:T(8,128)} %copy-done.2, s32[]{:T(128)S(6)} %select_n.8), kind=kOutput, calls=%fused_computation.8 | convolution fusion | flops 757983232 | bytes 5079048 | tf_op jit(solution)/shard_map/dot_general | solution.py:36
  (2 shorter events, 0.0 us)
Async XLA Ops:
  7.2 1.9 copy-start
  7.2 113.1 %all-reduce.3.cloned.1.call-start = ((), (), s32[]{:S(2)}) async-start(), calls=%async_computation | async-start | bytes 2031616 | tf_op jit(solution)/shard_map/psum | solution.py:21
  18.4 5.6 %copy-start.1 = (f32[1984,1984]{1,0:T(8,128)}, f32[1984,1984]{1,0:T(8,128)S(1)}, u32[]{:S(2)}) copy-start(f32[1984,1984]{1,0:T(8,128)S(1)} %convert_add_fusion) | copy-start | bytes 47235076
  39.3 217.4 %all-reduce.5.cloned.1.call-start = ((), (), s32[]{:S(2)}) async-start(), calls=%async_computation.1 | async-start | bytes 2031616 | tf_op jit(solution)/shard_map/psum | solution.py:31
  148.8 1.0 copy-start.2
  266.9 19.2 %copy-start.3 = (f32[1984,128]{1,0:T(8,128)S(1)}, f32[1984,128]{1,0:T(8,128)}, u32[]{:S(2)}) copy-start(f32[1984,128]{1,0:T(8,128)} %all-reduce.5.cloned.1.call-done) | copy-start | bytes 3047428
  267.0 19.2 %copy-start.4 = (f32[1,248,1984]{2,1,0:T(8,128)S(1)}, f32[1,248,1984]{2,1,0:T(8,128)}, u32[]{:S(2)}) copy-start(f32[1,248,1984]{2,1,0:T(8,128)} %param.8) | copy-start | bytes 5904388
Sparse Core Ops, SparseCore 0:
  39.4 80.8 all-reduce.2
  179.8 76.8 all-reduce.4
where the time goes:
time: 298 us; the launch traced here: 297 us
  waiting for transfers between devices  158 us (53%)
  matrix products  83.4 us (28%)
  other arithmetic  25.8 us (9%)
  between operations  14.8 us (5%)
  local copies, waits for them, and re-layouts  8.49 us (3%)
  blocking collectives  6.53 us (2%)
    psum x1, waiting for transfers between devices, per_device(): left_full = lax.psum(left_local, 'dp')  80.8 us
    psum x1, waiting for transfers between devices, per_device(): q_tile = lax.psum(right_local, 'dp') / replicas  77 us
    dot_general x1, matrix products, per_device(): lax.dot_general(merged, ortho_basis, (((0,), (0,)), ((), ())), precision=...  29.9 us
    dot_general x1, matrix products, per_device(): decoded = jnp.dot(ortho_basis, q_tile.T, precision=PRECISE)  19.2 us
    dot_general x1, matrix products, per_device(): left_local = jnp.dot(merged, warm_start, precision=PRECISE)  15.3 us
    another operation x3, other arithmetic, per_device(): cholesky_low = jnp.linalg.cholesky(gram_matrix)  12.4 us
    another operation x2, other arithmetic, per_device(): lax.linalg.triangular_solve(cholesky_low, left_full, left_side=False, low...  10.5 us
    dot_general x1, matrix products, per_device(): lax.dot_general(inputs, upstream, (((0,), (0,)), ((), ())), preferred_ele...  9.34 us
  transfers between devices with their start and end apart: 2, of which 2 were waited for; matrix products, arithmetic and copies ran while one was open for 0% of the time, Pallas kernels for 0%

commit v1 on v0

--- a/solution.py
+++ b/solution.py
@@ -8,6 +8,11 @@
 
 
 def per_device(acts, grads, error, momentum, q_start):
+
+    def end_works_over_axis(block_here):
+        local_part = lax.all_gather(block_here, axis_name="dp").sum(axis=0)
+        return local_part
+
     inputs = acts[:, 0, :]
     upstream = grads[:, 0, :]
     local_grad = lax.dot_general(
@@ -18,7 +23,7 @@
     replicas = lax.axis_size("dp")
     owned_rows = momentum.shape[1]
     left_local = jnp.dot(merged, warm_start, precision=PRECISE)
-    left_full = lax.psum(left_local, "dp")
+    left_full = end_works_over_axis(left_local)
     gram_matrix = jnp.dot(left_full.T, left_full, precision=PRECISE)
     cholesky_low = jnp.linalg.cholesky(gram_matrix)
     ortho_basis = lax.linalg.triangular_solve(

time: 298 us -> 345 us (1.16)
  waiting for transfers between devices: 158 us -> 200 us
  other arithmetic: 25.8 us -> 30.6 us
    all_gather x0 -> x1, waiting for transfers between devices: none -> 124 us  [end_works_over_axis(): local_part = lax.all_gather(block_here, axis_name='dp').sum(axis=0)]
    psum x1 -> x0, waiting for transfers between devices: 80.8 us -> none  [per_device(): left_full = lax.psum(left_local, 'dp')]
    reduce_sum x0 -> x1, other arithmetic: none -> 4.76 us  [end_works_over_axis(): local_part = lax.all_gather(block_here, axis_name='dp').sum(axis=0)]
where the time goes in v1:
time: 345 us; the launch traced here: 344 us
  waiting for transfers between devices  200 us (58%)
  matrix products  83.4 us (24%)
  other arithmetic  30.6 us (9%)
  between operations  14.8 us (4%)
  local copies, waits for them, and re-layouts  8.49 us (2%)
  blocking collectives  6.53 us (2%)
    all_gather x1, waiting for transfers between devices, end_works_over_axis(): local_part = lax.all_gather(block_here, axis_name='dp').sum(axis=0)  124 us
    psum x1, waiting for transfers between devices, per_device(): q_tile = lax.psum(right_local, 'dp') / replicas  76.4 us
    dot_general x1, matrix products, per_device(): lax.dot_general(merged, ortho_basis, (((0,), (0,)), ((), ())), precision=...  29.9 us
    dot_general x1, matrix products, per_device(): decoded = jnp.dot(ortho_basis, q_tile.T, precision=PRECISE)  19.2 us
    dot_general x1, matrix products, per_device(): left_local = jnp.dot(merged, warm_start, precision=PRECISE)  15.3 us
    another operation x3, other arithmetic, per_device(): cholesky_low = jnp.linalg.cholesky(gram_matrix)  12.4 us
    another operation x2, other arithmetic, per_device(): lax.linalg.triangular_solve(cholesky_low, left_full, left_side=False, low...  10.5 us
    dot_general x1, matrix products, per_device(): lax.dot_general(inputs, upstream, (((0,), (0,)), ((), ())), preferred_ele...  9.34 us
  transfers between devices with their start and end apart: 2, of which 2 were waited for; matrix products, arithmetic and copies ran while one was open for 0% of the time, Pallas kernels for 0%

profile of v1, /device:TPU:0, one launch (start us, length us, event | category | flops | bytes accessed | tf_op | source)
XLA Modules:
  0.0 344.4 jit_solution(2979810261962262247)
XLA Ops:
  7.2 0.0 copy-start
  7.2 0.0 all-gather.3.cloned.1.call-start
  7.2 1.8 copy-done
  9.0 9.3 %convert_add_fusion = f32[1984,1984]{1,0:T(8,128)S(1)} fusion(bf16[1,1,1984,1984]{3,2,1,0:T(8,128)(2,1)} %param.7, bf16[768,1,1984]{0,2,1:T(8,128)(2,1)S(1)} %copy-done, bf16[768,1,1984]{0,2,1:T(8,128)(2,1)} %param.5), kind=kOutput, calls=%fused_computation | convolution fusion | flops 6053961728 | bytes 29712384 | tf_op jit(solution)/shard_map/dot_general | solution.py:18
  18.4 0.0 copy-start.1
  18.4 5.6 %copy-done.1 = f32[1984,1984]{1,0:T(8,128)} copy-done((f32[1984,1984]{1,0:T(8,128)}, f32[1984,1984]{1,0:T(8,128)S(1)}, u32[]{:S(2)}) %copy-start.1) | copy-done | bytes 15745048
  24.0 15.3 %fusion.6 = f32[1984,128]{1,0:T(8,128)} fusion(f32[1984,1984]{1,0:T(8,128)S(1)} %convert_add_fusion, f32[1,1984,128]{2,1,0:T(8,128)} %param.9), kind=kOutput, calls=%fused_computation.9 | convolution fusion | flops 6046089216 | bytes 17776640 | tf_op jit(solution)/shard_map/dot_general | solution.py:25
  39.3 0.0 all-gather.3.cloned.1.call-update
  39.3 0.2 all-reduce.2.cloned.1.call-start
  39.6 123.8 %all-gather.3.cloned.1.call-done = f32[15872,128]{1,0:T(8,128)} async-done(((f32[1984,128]{1,0:T(8,128)}), f32[15872,128]{1,0:T(8,128)}) %all-gather.3.cloned.1.call-update) | async-done | bytes 8126480 | tf_op jit(solution)/shard_map/all_gather | solution.py:13
  163.3 4.8 %reduce_sum.18 = f32[1984,128]{1,0:T(8,128)} reduce(f32[8,1984,128]{2,1,0:T(8,128)} %bitcast.37, f32[]{:T(128)} %constant.52.clone.1), dimensions={0}, to_apply=%region_0.0 | reduce | flops 1777664 | bytes 9142276 | tf_op jit(solution)/shard_map/reduce_sum | solution.py:13
  168.1 3.3 fusion.20
  171.4 0.1 copy.8
  171.6 11.7 %cholesky.16 = f32[128,128]{1,0:T(8,128)S(1)} custom-call(f32[128,128]{1,0:T(8,128)S(1)} %fusion.16), custom_call_target="Cholesky" | custom-call | tf_op jit(solution)/shard_map/jit(cholesky)/cholesky | solution.py:28
  183.3 0.6 compare_reduce_fusion
  183.9 0.7 fusion.13
  184.6 9.8 %custom-call.6 = f32[1,128,128]{1,2,0:T(8,128)S(1)} custom-call(f32[1,128,128]{2,1,0:T(8,128)S(1)} %fusion.13), custom_call_target="InvertDiagBlocksLowerTriangular" | custom-call | tf_op jit(solution)/shard_map/triangular_solve | solution.py:29
  194.4 2.2 fusion.14
  196.6 0.0 copy-start.2
  196.6 1.0 copy-done.2
  197.6 29.9 %fusion.21 = f32[1984,128]{1,0:T(8,128)} fusion(f32[1984,1984]{1,0:T(8,128)} %copy-done.1, f32[1984,128]{1,0:T(8,128)S(1)} %fusion.14), kind=kOutput, calls=%fused_computation.32 | convolution fusion | flops 6046089216 | bytes 17776640 | tf_op jit(solution)/shard_map/dot_general | solution.py:35
  227.5 0.0 all-reduce.2.cloned.1.call-update
  227.5 76.4 %all-reduce.2.cloned.1.call-done = f32[1984,128]{1,0:T(8,128)} async-done(((f32[1984,128]{1,0:T(8,128)}), f32[1984,128]{1,0:T(8,128)}) %all-reduce.2.cloned.1.call-update) | async-done | bytes 1015824 | tf_op jit(solution)/shard_map/psum | solution.py:36
  303.9 3.0 multiply_bitcast_fusion
  306.9 6.5 %psum.15 = f32[]{:T(128)} all-reduce(f32[]{:T(128)} %get-tuple-element.4), channel_id=1, replica_groups=mesh['dp'=8,'mp'=4] {'mp'}, use_global_device_ids=true, to_apply=%region_5.6 | all-reduce | flops 1 | bytes 8 | tf_op jit(solution)/shard_map/psum | solution.py:37
  314.1 0.0 copy-start.3
  314.1 0.0 copy-start.4
  314.1 19.2 %fusion = bf16[1,1,1984,1984]{3,2,1,0:T(8,128)(2,1)} fusion(f32[1984,1984]{1,0:T(8,128)} %copy-done.1, f32[1984,128]{1,0:T(8,128)} %copy-done.2, f32[1984,128]{1,0:T(8,128)} %all-reduce.2.cloned.1.call-done), kind=kOutput, calls=%fused_computation.2 | convolution fusion | flops 6054215680 | bytes 25649152 | tf_op jit(solution)/shard_map/dot_general | solution.py:39
  333.3 0.0 copy-done.3
  333.3 0.0 copy-done.4
  333.3 4.2 %fusion.5 = f32[1,248,1984]{2,1,0:T(8,128)} fusion(f32[1,248,1984]{2,1,0:T(8,128)S(1)} %copy-done.4, f32[]{:T(128)S(6)} %add.30, f32[1984,128]{1,0:T(8,128)S(1)} %copy-done.3, f32[1984,128]{1,0:T(8,128)} %copy-done.2, s32[]{:T(128)S(6)} %select_n.8), kind=kOutput, calls=%fused_computation.8 | convolution fusion | flops 757983232 | bytes 5079048 | tf_op jit(solution)/shard_map/dot_general | solution.py:41
  (2 shorter events, 0.0 us)
Async XLA Ops:
  7.2 1.9 copy-start
  7.2 156.2 %all-gather.3.cloned.1.call-start = ((), (), s32[]{:S(2)}) async-start(), calls=%async_computation.1 | async-start | bytes 9142272 | tf_op jit(solution)/shard_map/all_gather | solution.py:13
  18.4 5.6 %copy-start.1 = (f32[1984,1984]{1,0:T(8,128)}, f32[1984,1984]{1,0:T(8,128)S(1)}, u32[]{:S(2)}) copy-start(f32[1984,1984]{1,0:T(8,128)S(1)} %convert_add_fusion) | copy-start | bytes 47235076
  39.3 264.6 %all-reduce.2.cloned.1.call-start = ((), (), s32[]{:S(2)}) async-start(), calls=%async_computation | async-start | bytes 2031616 | tf_op jit(solution)/shard_map/psum | solution.py:36
  196.6 1.0 copy-start.2
  314.1 19.2 %copy-start.3 = (f32[1984,128]{1,0:T(8,128)S(1)}, f32[1984,128]{1,0:T(8,128)}, u32[]{:S(2)}) copy-start(f32[1984,128]{1,0:T(8,128)} %all-reduce.2.cloned.1.call-done) | copy-start | bytes 3047428
  314.1 19.2 %copy-start.4 = (f32[1,248,1984]{2,1,0:T(8,128)S(1)}, f32[1,248,1984]{2,1,0:T(8,128)}, u32[]{:S(2)}) copy-start(f32[1,248,1984]{2,1,0:T(8,128)} %param.8) | copy-start | bytes 5904388
Sparse Core Ops, SparseCore 0:
  39.4 123.8 all-gather.2
  227.6 76.2 all-reduce.1
